TPU v7x, 32 devices: a whole 2x2x4 slice. The times are simulated.
32 devices in a mesh: lat: 8 (over y, x, core), lon: 4 (over z).
Axes of the slice: x: 2, y: 2, z: 4, core: 2. Of those that a mesh axis runs over, the one named last changes fastest.
Arguments:
- coeffs_old: float32 [640, 2, 3, 50, 640], P(('lat', 'lon')), may hold values from -0.16 to 0.16
- noise: bfloat16 [640, 2, 3, 50, 640], P(('lat', 'lon')), may hold values from -6 to 6
- legendre: float32 [640, 640, 640], P(('lat', 'lon')), may hold values from -0.25 to 0.25
- decay: float32 [3], replicated, may hold values from 0.3 to 0.97
- amplitude: float32 [3, 640], replicated, may hold values from 0.005 to 0.05
- wavenumber_of_slot: int32 [640], replicated, may hold values from 0 to 639, as said below
- lat_order: int32 [640], replicated, may hold values from 0 to 639, each once
Outputs:
- coeffs_new: float32 [640, 2, 3, 50, 640], P(('lat', 'lon'))
- pattern: float32 [640, 50, 1280], P(('lat', 'lon'))
Inputs may be any that keep to these rules, and one draw needn't show every extreme that they name: `wavenumber_of_slot`: every wavenumber fills exactly one slot; the sums of the wavenumbers of one device's 20 slots differ between devices by less than 32. `lat_order`: every latitude stands in exactly one row.
All inputs are finite; a program needn't handle non-finite values.
Results may differ from a plain program's by a relative error of at most 0.0003.
Values sent between devices are 32-bit elements; how exact they have to be, the bound alone decides.
A program may use at most 192 MiB of HBM per device.

v0:
```python
import jax
import jax.numpy as jnp
from jax import lax
from jax.sharding import PartitionSpec as P

LON = 1280


TWO_PI = 6.283185307179586


def evolve(coeffs_old, noise, decay, amplitude, waves):
    width = coeffs_old.shape[4]
    offsets = lax.broadcasted_iota(jnp.int32, (waves.shape[0], width), 1)
    live = waves[:, None] + offsets < width
    padded = jnp.concatenate([amplitude, jnp.zeros_like(amplitude)], axis=1)
    spread = jax.vmap(lambda wave: lax.dynamic_slice_in_dim(padded, wave, width, 1))(waves)
    factor = jnp.sqrt(1.0 - decay * decay)
    fresh = decay[None, None, :, None, None] * coeffs_old + (spread * factor[None, :, None])[
        :, None, :, None, :
    ] * noise.astype(jnp.float32)
    return jnp.where(live[:, None, None, None, :], fresh, jnp.zeros_like(fresh))


def synthesis_table(waves, length):
    column = lax.broadcasted_iota(jnp.int32, (waves.shape[0], length), 1)
    phase = waves[:, None] * column % length
    angle = phase.astype(jnp.float32) * (TWO_PI / length)
    weight = jnp.where(waves == 0, 1.0, 2.0).astype(jnp.float32)[:, None]
    return jnp.stack([weight * jnp.cos(angle), -weight * jnp.sin(angle)], axis=1)


def synthesize(values, table):
    return jnp.einsum("sreq,srl->qel", values, table, precision=lax.Precision.HIGHEST)


def local(coeffs_old, noise, legendre, decay, amplitude, wavenumber_of_slot, lat_order):
    lat_count = lax.axis_size("lat")
    lon_count = lax.axis_size("lon")
    lat_index = lax.axis_index("lat")
    lon_index = lax.axis_index("lon")
    slots = coeffs_old.shape[0]
    mine = lax.dynamic_slice_in_dim(
        wavenumber_of_slot, (lat_index * lon_count + lon_index) * slots, slots
    )
    coeffs_new = evolve(coeffs_old, noise, decay, amplitude, mine)
    field = jnp.einsum("srkej,slj->srel", coeffs_new, legendre, precision=lax.Precision.HIGHEST)
    field = jnp.take(field, lat_order, axis=3)
    ordered = wavenumber_of_slot.reshape(lat_count, lon_count, slots).transpose(1, 0, 2).reshape(-1)
    full_table = synthesis_table(ordered, LON)
    pattern = synthesize(
        lax.all_to_all(
            lax.all_to_all(field, "lat", split_axis=3, concat_axis=0, tiled=True),
            "lon",
            split_axis=3,
            concat_axis=0,
            tiled=True,
        ),
        full_table,
    )
    return (coeffs_new, pattern)


def solution(mesh):
    in_specs = (
        P(("lat", "lon"), None, None, None, None),
        P(("lat", "lon"), None, None, None, None),
        P(("lat", "lon"), None, None),
        P(),
        P(),
        P(),
        P(),
    )
    out_specs = (P(("lat", "lon"), None, None, None, None), P(("lat", "lon"), None, None))
    return jax.shard_map(local, mesh=mesh, in_specs=in_specs, out_specs=out_specs, check_vma=False)
```

profile of v0, /device:TPU:0, one launch (start us, length us, event | category | flops | bytes accessed | tf_op | source)
XLA Modules:
  0.0 590.6 jit_solution(11389839738425668350)
XLA Ops:
  2.0 0.8 fusion.12
  3.5 26.4 %while.1 = (s32[]{:T(128)}, f32[3,1280]{1,0:T(4,128)S(1)}, s32[20,2]{0,1:T(2,128)S(1)}, f32[20,3,640]{2,1,0:T(4,128)S(1)}, s32[]{:T(128)}) while((s32[]{:T(128)}, f32[3,1280]{1,0:T(4,128)S(1)}, s32[20,2]{0,1:T(2,128)S(1)}, f32[20,3,640]{2,1,0:T(4,128)S(1)}, s32[]{:T(128)}) %tuple.24), condition=%wide.while_cond, body=%wide.while_body.sunk | while | flops 2 | bytes 20585 | solution.py:17
  4.1 0.7 bitcast_dynamic-update-slice_fusion.2
  5.4 0.7 bitcast_dynamic-update-slice_fusion.2
  6.7 0.7 bitcast_dynamic-update-slice_fusion.2
  8.1 0.7 bitcast_dynamic-update-slice_fusion.2
  9.4 0.7 bitcast_dynamic-update-slice_fusion.2
  10.7 0.7 bitcast_dynamic-update-slice_fusion.2
  12.0 0.7 bitcast_dynamic-update-slice_fusion.2
  13.3 0.7 bitcast_dynamic-update-slice_fusion.2
  14.7 0.7 bitcast_dynamic-update-slice_fusion.2
  16.0 0.7 bitcast_dynamic-update-slice_fusion.2
  17.3 0.7 bitcast_dynamic-update-slice_fusion.2
  18.6 0.7 bitcast_dynamic-update-slice_fusion.2
  30.8 32.2 %fusion.15 = (f32[20,2,50,640]{3,1,2,0:T(2,128)}, f32[20,2,3,50,640]{4,1,3,2,0:T(2,128)}) fusion(bf16[20,2,3,50,640]{4,1,3,2,0:T(2,128)(2,1)} %param.8, f32[20,3,640]{2,1,0:T(4,128)S(1)} %broadcast_multiply_fusion, f32[20,2,3,50,640]{4,1,3,2,0:T(2,128)} %param.7, f32[3]{0:T(128)} %param.10, pred[20,640]{1,0:T(8,128)(4,1)S(1)} %add_compare_fusion), kind=kLoop, calls=%fused_computation.33 | loop fusion | flops 21760000 | bytes 43686412 | tf_op jit(solution)/shard_map/srkej,slj->srel/reduce_sum | solution.py:47
  63.0 36.1 %fusion = f32[20,2,50,640]{3,2,1,0:T(8,128)} fusion(f32[20,640,640]{2,1,0:T(8,128)} %param.9, f32[20,2,50,640]{3,1,2,0:T(2,128)} %get-tuple-element.18), kind=kOutput, calls=%fused_computation.3 | convolution fusion | flops 9830400000 | bytes 43008000 | tf_op jit(solution)/shard_map/srkej,slj->srel/dot_general | solution.py:47
  99.1 15.9 %copy.33 = f32[20,2,50,640]{2,1,3,0:T(2,128)} copy(f32[20,2,50,640]{3,2,1,0:T(8,128)} %fusion) | data formatting | bytes 10240000 | tf_op jit(solution)/shard_map/srkej,slj->srel/dot_general | solution.py:47
  115.0 38.6 %gather_fusion = f32[640,20,2,50]{3,2,1,0:T(2,128)} fusion(f32[20,2,50,640]{2,1,3,0:T(2,128)} %copy.33, s32[1024]{0:T(1024)S(1)} %pad_clamp_fusion), kind=kCustom, calls=%fused_computation | custom fusion | bytes 10242560 | tf_op jit(solution)/shard_map/jit(_take)/gather | solution.py:48
  153.6 10.2 %fusion.16 = f32[640,20,2,50]{3,2,1,0:T(2,128)} fusion(f32[640,20,2,50]{3,2,1,0:T(2,128)} %gather_fusion, pred[640]{0:T(1024)(128)(4,1)S(1)} %compare_and_fusion), kind=kLoop, calls=%fused_computation.34 | loop fusion | flops 1280000 | bytes 10240640
  163.8 27.8 %reshape.218 = f32[8,1,160000]{2,1,0:T(1,128)} reshape(f32[640,20,2,50]{3,2,1,0:T(2,128)} %fusion.16) | data formatting | bytes 10240000
  191.5 64.3 %all_to_all.36 = f32[8,1,160000]{2,1,0:T(1,128)} all-to-all(f32[8,1,160000]{2,1,0:T(1,128)} %reshape.218), channel_id=1, replica_groups=mesh['lat'=8,'lon'=4] {'lat'}, dimensions={0} | all-to-all | bytes 10240000 | tf_op jit(solution)/shard_map/all_to_all | solution.py:53
  256.3 17.0 %reduce = f32[8,160000]{1,0:T(8,128)} reduce(f32[8,1,160000]{2,1,0:T(1,128)} %all_to_all.36, f32[]{:T(128)} %broadcast.203), dimensions={1}, to_apply=%all_to_all.26.reduce_sub_computation | reduce | bytes 10240004 | tf_op jit(solution)/shard_map/all_to_all | solution.py:53
  273.3 33.3 %reshape.219 = f32[640,20,2,50]{3,2,1,0:T(2,128)} reshape(f32[8,160000]{1,0:T(8,128)} %reduce) | data formatting | bytes 10240000
  306.6 17.1 %copy.42 = f32[20,2,50,8,80]{4,3,1,2,0:T(8,128)} copy(f32[20,2,50,8,80]{2,1,0,4,3:T(2,128)} %bitcast.41) | data formatting | bytes 10240000 | tf_op jit(solution)/shard_map/all_to_all | solution.py:53
  323.7 13.0 %copy.35 = f32[8,20,2,50,80]{4,2,3,1,0:T(2,128)} copy(f32[8,20,2,50,80]{4,0,2,3,1:T(8,128)} %bitcast.43) | data formatting | bytes 10240000 | tf_op jit(solution)/shard_map/all_to_all | solution.py:53
  336.7 18.0 %copy.36 = f32[160,2,50,80]{0,1,2,3:T(2,128)} copy(f32[160,2,50,80]{3,1,2,0:T(2,128)} %bitcast.42) | data formatting | bytes 10240000 | tf_op jit(solution)/shard_map/all_to_all | solution.py:53
  354.7 5.7 all-to-all-start.1
  360.7 15.2 %cosine_multiply_fusion = (f32[640,1,1280]{2,0,1:T(8,128)S(1)}, f32[640,1,1280]{2,0,1:T(8,128)}) fusion(s32[640]{0:T(1024)S(1)} %reshape.185, f32[640]{0:T(1024)S(1)} %get-tuple-element.24, f32[640]{0:T(1024)S(1)} %get-tuple-element.25), kind=kLoop, calls=%fused_computation.17 | loop fusion | flops 9011200 | bytes 6561280 | tf_op jit(solution)/shard_map/mul | solution.py:30
  375.9 164.0 %all-to-all-done.1 = f32[160,2,50,80]{0,1,2,3:T(2,128)} async-done(((f32[160,2,50,80]{0,1,2,3:T(2,128)}), f32[160,2,50,80]{0,1,2,3:T(2,128)}, u32[]{:S(2)}, u32[]{:S(2)}) %all-to-all-start.1) | async-done | bytes 5120032 | tf_op jit(solution)/shard_map/all_to_all | solution.py:52
  539.9 11.8 %copy.44 = f32[4,160,2,50,20]{1,0,3,2,4:T(4,128)} copy(f32[4,160,2,50,20]{1,2,3,4,0:T(2,128)} %bitcast.11) | data formatting | bytes 10240000 | tf_op jit(solution)/shard_map/all_to_all | solution.py:52
  551.7 9.5 %reshape.217 = f32[640,2,50,20]{0,2,1,3:T(8,128)} reshape(f32[4,160,2,50,20]{1,0,3,2,4:T(4,128)} %copy.44) | data formatting | bytes 10240000 | tf_op jit(solution)/shard_map/all_to_all | solution.py:52
  561.3 29.1 %fusion.6 = f32[20,50,1280]{2,1,0:T(8,128)} fusion(f32[640,2,50,20]{0,2,1,3:T(8,128)} %reshape.217, f32[640,1,1280]{2,0,1:T(8,128)} %get-tuple-element.23, f32[640,1,1280]{2,0,1:T(8,128)S(1)} %get-tuple-element.22), kind=kOutput, calls=%fused_computation.13 | convolution fusion | flops 19662438400 | bytes 16793600 | tf_op jit(solution)/shard_map/sreq,srl->qel/dot_general | solution.py:34
  (64 shorter events, 21.3 us)
Async XLA Ops:
  354.7 5.8 copy-start
  354.7 185.2 %all-to-all-start.1 = ((f32[160,2,50,80]{0,1,2,3:T(2,128)}), f32[160,2,50,80]{0,1,2,3:T(2,128)}, u32[]{:S(2)}, u32[]{:S(2)}) async-start(f32[160,2,50,80]{0,1,2,3:T(2,128)} %copy.36), calls=%async_computation.1 | async-start | bytes 16384000 | tf_op jit(solution)/shard_map/all_to_all | solution.py:52
where the time goes:
time: 601 us; the launch traced here: 591 us
  local copies, waits for them, and re-layouts  213 us (35%)
  waiting for transfers between devices  164 us (27%)
  other arithmetic  77.6 us (13%)
  matrix products  65.2 us (11%)
  blocking collectives  64.3 us (11%)
    all_to_all x1, waiting for transfers between devices, local(): lax.all_to_all(lax.all_to_all(field, 'lat', split_axis=3, concat_axis=0,...  164 us
    all_to_all x1, blocking collectives, local(): lax.all_to_all(field, 'lat', split_axis=3, concat_axis=0, tiled=True)  64.3 us
    unnamed x4, local copies, waits for them, and re-layouts  61.1 us
    all_to_all x4, local copies, waits for them, and re-layouts, local(): lax.all_to_all(field, 'lat', split_axis=3, concat_axis=0, tiled=True)  48.6 us
    gather x1, local copies, waits for them, and re-layouts, local(): field = jnp.take(field, lat_order, axis=3)  38.6 us
    dot_general x1, matrix products, local(): jnp.einsum('srkej,slj->srel', coeffs_new, legendre, precision=lax.Precisi...  36.1 us
    reduce_sum x1, other arithmetic, local(): jnp.einsum('srkej,slj->srel', coeffs_new, legendre, precision=lax.Precisi...  32.2 us
    dot_general x1, matrix products, synthesize(): jnp.einsum('sreq,srl->qel', values, table, precision=lax.Precision.HIGHEST)  29.1 us
  transfers between devices with their start and end apart: 1, of which 1 were waited for; matrix products, arithmetic and copies ran while one was open for 3% of the time, Pallas kernels for 0%

commit v1 on v0

v1 whole, which is shorter than its diff:
```python
import functools

import jax
import jax.numpy as jnp
from jax import lax
from jax.experimental import pallas as pl
from jax.experimental.pallas import tpu as pltpu
from jax.sharding import PartitionSpec as P

TWO_PI = 6.283185307179586
LANES = 128


def group_size(slots):
    return 4 if slots % 4 == 0 else slots


def split(x):
    high = x.astype(jnp.bfloat16)
    return high, (x - high.astype(jnp.float32)).astype(jnp.bfloat16)


def factors(decay, amplitude, waves):
    width = amplitude.shape[1]
    offsets = lax.broadcasted_iota(jnp.int32, (waves.shape[0], width), 1)
    live = (waves[:, None] + offsets < width).astype(jnp.float32)
    padded = jnp.concatenate([amplitude, jnp.zeros_like(amplitude)], axis=1)
    spread = jax.vmap(lambda wave: lax.dynamic_slice_in_dim(padded, wave, width, 1))(waves)
    fresh = spread * jnp.sqrt(1.0 - decay * decay)[None, :, None] * live[:, None, :]
    keep = decay[None, :, None] * live[:, None, :]
    return keep, fresh


def transform_kernel(order_ref, old_ref, noise_ref, basis_ref, keep_ref, fresh_ref, new_ref, send_ref, weights, field):
    group, step = pl.num_programs(1), pl.program_id(1)
    scales, members = old_ref.shape[2], old_ref.shape[3]
    devices, rows, wide = send_ref.shape[1:]
    lat_dev = order_ref.shape[0] // devices

    @pl.when((pl.program_id(0) == 0) & (step == 0))
    def _():
        weights[...] = jnp.zeros_like(weights)

    for part in range(2):
        total = None
        for scale in range(scales):
            keep = keep_ref[0, scale : scale + 1, :]
            fresh = fresh_ref[0, scale : scale + 1, :]
            value = keep * old_ref[0, part, scale] + fresh * noise_ref[0, part, scale].astype(jnp.float32)
            new_ref[0, part, scale] = value
            total = value if total is None else total + value
        weights[part * 64 : part * 64 + members, :] = total
    high, low = split(weights[...])
    both = jnp.concatenate([high, low], axis=0)
    basis_high, basis_low = split(basis_ref[0])
    contract = (((1,), (1,)), ((), ()))
    first = lax.dot_general(basis_high, both, contract, preferred_element_type=jnp.float32)
    second = lax.dot_general(basis_low, high, contract, preferred_element_type=jnp.float32)
    product = first[:, :LANES] + first[:, LANES:] + second
    other = pltpu.roll(product, 64, axis=1)
    for index in range(rows // 2):

        @pl.when(step == index)
        def _(index=index):
            field[:, 2 * index, :] = product
            field[:, 2 * index + 1, :] = other

    @pl.when(step == group - 1)
    def _():
        lane = lax.broadcasted_iota(jnp.int32, (rows, LANES), 1)

        def pack(device, carry):
            tiles = [jnp.zeros((rows, LANES), jnp.float32) for _ in range(wide // LANES)]
            for q in range(lat_dev):
                piece = field[order_ref[device * lat_dev + q]]
                start = members * q
                offset = start % LANES
                if offset:
                    piece = pltpu.roll(piece, offset, axis=1)
                tile = start // LANES
                tiles[tile] = jnp.where((lane >= offset) & (lane < offset + members), piece, tiles[tile])
                if offset + members > LANES:
                    tiles[tile + 1] = jnp.where(lane < offset + members - LANES, piece, tiles[tile + 1])
            for index, tile in enumerate(tiles):
                send_ref[0, device, :, index * LANES : (index + 1) * LANES] = tile
            return carry

        lax.fori_loop(0, devices, pack, 0)


def transform(coeffs_old, noise, legendre, keep, fresh, lat_order, devices):
    slots, parts, scales, members, width = coeffs_old.shape
    lats = legendre.shape[1]
    group = group_size(slots)
    rows = group * parts
    wide = -(-(lats // devices * members) // LANES) * LANES

    def slot5(g, i, order):
        return (g * group + i, 0, 0, 0, 0)

    def slot3(g, i, order):
        return (g * group + i, 0, 0)

    spec = pltpu.PrefetchScalarGridSpec(
        num_scalar_prefetch=1,
        grid=(slots // group, group),
        in_specs=[
            pl.BlockSpec((1, parts, scales, members, width), slot5),
            pl.BlockSpec((1, parts, scales, members, width), slot5),
            pl.BlockSpec((1, lats, width), slot3),
            pl.BlockSpec((1, scales, width), slot3),
            pl.BlockSpec((1, scales, width), slot3),
        ],
        out_specs=[
            pl.BlockSpec((1, parts, scales, members, width), slot5),
            pl.BlockSpec((1, devices, rows, wide), lambda g, i, order: (g, 0, 0, 0)),
        ],
        scratch_shapes=[
            pltpu.VMEM((LANES, width), jnp.float32),
            pltpu.VMEM((lats, rows, LANES), jnp.float32),
        ],
    )
    return pl.pallas_call(
        transform_kernel,
        grid_spec=spec,
        out_shape=[
            jax.ShapeDtypeStruct(coeffs_old.shape, jnp.float32),
            jax.ShapeDtypeStruct((slots // group, devices, rows, wide), jnp.float32),
        ],
        compiler_params=pltpu.CompilerParams(dimension_semantics=("arbitrary", "arbitrary")),
    )(lat_order, coeffs_old, noise, legendre, keep, fresh)


def synthesis_table(waves, length):
    column = lax.broadcasted_iota(jnp.int32, (waves.shape[0], length), 1)
    phase = waves[:, None] * column % length
    angle = phase.astype(jnp.float32) * (TWO_PI / length)
    weight = jnp.where(waves == 0, 1.0, 2.0).astype(jnp.float32)[:, None]
    return jnp.stack([weight * jnp.cos(angle), -weight * jnp.sin(angle)], axis=1).reshape(-1, length)


def local(coeffs_old, noise, legendre, decay, amplitude, wavenumber_of_slot, lat_order):
    devices = lax.axis_size("lat") * lax.axis_size("lon")
    me = lax.axis_index("lat") * lax.axis_size("lon") + lax.axis_index("lon")
    slots, parts, scales, members, width = coeffs_old.shape
    lats = legendre.shape[1]
    lons = 2 * lats
    lat_dev = lats // devices
    group = group_size(slots)
    mine = lax.dynamic_slice_in_dim(wavenumber_of_slot, me * slots, slots)
    keep, fresh = factors(decay, amplitude, mine)
    coeffs_new, send = transform(coeffs_old, noise, legendre, keep, fresh, lat_order, devices)
    got = lax.all_to_all(send, ("lat", "lon"), split_axis=1, concat_axis=1, tiled=True)
    ordered = wavenumber_of_slot.reshape(devices, slots // group, group).transpose(1, 0, 2).reshape(-1)
    table = synthesis_table(ordered, lons)
    values = got.reshape(-1, got.shape[-1])
    out = lax.dot_general(values, table, (((0,), (0,)), ((), ())), precision=lax.Precision.HIGH)
    pattern = out[: lat_dev * members].reshape(lat_dev, members, lons)
    return (coeffs_new, pattern)


def solution(mesh):
    split_rows = ("lat", "lon")
    in_specs = (
        P(split_rows, None, None, None, None),
        P(split_rows, None, None, None, None),
        P(split_rows, None, None),
        P(),
        P(),
        P(),
        P(),
    )
    out_specs = (P(split_rows, None, None, None, None), P(split_rows, None, None))
    return jax.shard_map(local, mesh=mesh, in_specs=in_specs, out_specs=out_specs, check_vma=False)
```

time: 601 us -> 260 us (0.43); the launches traced: 591 us -> 258 us
  waiting for transfers between devices: 164 us -> 54.8 us
  local copies, waits for them, and re-layouts: 213 us -> 106 us
  blocking collectives: 64.3 us -> 0 us
  other arithmetic: 77.6 us -> 19.6 us
  Pallas kernels: 0 us -> 54.3 us
  matrix products: 65.2 us -> 14.2 us
    all_to_all x1, waiting for transfers between devices: 164 us -> 54.8 us  [local(): lax.all_to_all(send, ('lat', 'lon'), split_axis=1, concat_axis=1, tiled=T...]
    all_to_all x6 -> x1, local copies, waits for them, and re-layouts: 69.9 us -> 3.32 us  [local(): lax.all_to_all(send, ('lat', 'lon'), split_axis=1, concat_axis=1, tiled=T...]
    all_to_all x1 -> x0, blocking collectives: 64.3 us -> none  [local(): lax.all_to_all(field, 'lat', split_axis=3, concat_axis=0, tiled=True)]
    pallas_call x0 -> x1, Pallas kernels: none -> 54.3 us  [transform(): pl.pallas_call(transform_kernel, grid_spec=spec, out_shape=[jax.ShapeDtyp...]
    dot_general x2 -> x1, matrix products: 65.2 us -> 14.2 us  [local(): lax.dot_general(values, table, (((0,), (0,)), ((), ())), precision=lax.Pr...]
    gather x61 -> x60, local copies, waits for them, and re-layouts: 65 us -> 26.4 us  [the longest x1 38.6 us: local(): field = jnp.take(field, lat_order, axis=3)]
    reduce_sum x1 -> x0, other arithmetic: 32.2 us -> none  [local(): jnp.einsum('srkej,slj->srel', coeffs_new, legendre, precision=lax.Precisi...]
    unnamed x4 -> x9, local copies, waits for them, and re-layouts: 61.1 us -> 44 us
  transfers between devices with their start and end apart: 1 -> 1, of which waited for: 1 -> 1; matrix products, arithmetic and copies ran while one was open for 3% -> 23% of each run, Pallas kernels for 0% -> 0%
where the time goes in v1:
time: 260 us; the launch traced here: 258 us
  local copies, waits for them, and re-layouts  106 us (41%)
  waiting for transfers between devices  54.8 us (21%)
  Pallas kernels  54.3 us (21%)
  other arithmetic  19.6 us (8%)
  matrix products  14.2 us (5%)
  starting transfers between devices  7.63 us (3%)
    all_to_all x1, waiting for transfers between devices, local(): lax.all_to_all(send, ('lat', 'lon'), split_axis=1, concat_axis=1, tiled=T...  54.8 us
    pallas_call x1, Pallas kernels, transform(): pl.pallas_call(transform_kernel, grid_spec=spec, out_shape=[jax.ShapeDtyp...  54.3 us
    unnamed x9, local copies, waits for them, and re-layouts  44 us
    gather x60, local copies, waits for them, and re-layouts  26.4 us
    dot_general x1, matrix products, local(): lax.dot_general(values, table, (((0,), (0,)), ((), ())), precision=lax.Pr...  14.2 us
    mul x1, other arithmetic, synthesis_table(): weight * jnp.cos(angle)  14 us
    another operation x1, local copies, waits for them, and re-layouts, synthesis_table(): jnp.stack([weight * jnp.cos(angle), -weight * jnp.sin(angle)], axis=1)  10.7 us
    reshape x1, local copies, waits for them, and re-layouts, synthesis_table(): jnp.stack([weight * jnp.cos(angle), -weight * jnp.sin(angle)], axis=1)  8.66 us
  transfers between devices with their start and end apart: 1, of which 1 were waited for; matrix products, arithmetic and copies ran while one was open for 23% of the time, Pallas kernels for 0%

profile of v1, /device:TPU:0, one launch (start us, length us, event | category | flops | bytes accessed | tf_op | source)
XLA Modules:
  0.0 257.5 jit_solution(16489514256234826594)
XLA Ops:
  0.6 0.8 fusion.8
  2.1 26.4 %while.1 = (s32[]{:T(128)}, f32[3,1280]{1,0:T(4,128)S(1)}, s32[20,2]{0,1:T(2,128)S(1)}, f32[20,3,640]{2,1,0:T(4,128)S(1)}, s32[]{:T(128)}) while((s32[]{:T(128)}, f32[3,1280]{1,0:T(4,128)S(1)}, s32[20,2]{0,1:T(2,128)S(1)}, f32[20,3,640]{2,1,0:T(4,128)S(1)}, s32[]{:T(128)}) %tuple.30), condition=%wide.while_cond, body=%wide.while_body.sunk | while | flops 2 | bytes 20577 | solution.py:28
  2.7 0.7 bitcast_dynamic-update-slice_fusion.2
  4.0 0.7 bitcast_dynamic-update-slice_fusion.2
  5.4 0.7 bitcast_dynamic-update-slice_fusion.2
  6.7 0.7 bitcast_dynamic-update-slice_fusion.2
  8.0 0.7 bitcast_dynamic-update-slice_fusion.2
  9.3 0.7 bitcast_dynamic-update-slice_fusion.2
  10.6 0.7 bitcast_dynamic-update-slice_fusion.2
  12.0 0.7 bitcast_dynamic-update-slice_fusion.2
  13.3 0.7 bitcast_dynamic-update-slice_fusion.2
  14.6 0.7 bitcast_dynamic-update-slice_fusion.2
  15.9 0.7 bitcast_dynamic-update-slice_fusion.2
  17.2 0.7 bitcast_dynamic-update-slice_fusion.2
  18.6 0.7 bitcast_dynamic-update-slice_fusion.2
  22.5 0.7 bitcast_dynamic-update-slice_fusion.2
  29.3 12.5 %copy.33.old_ref = f32[20,2,3,50,640]{4,3,2,1,0:T(8,128)} copy(f32[20,2,3,50,640]{4,1,3,2,0:T(2,128)} %param.7) | data formatting | bytes 30720000 | tf_op args[0]
  41.8 7.8 %copy.34.noise_ref = bf16[20,2,3,50,640]{4,3,2,1,0:T(8,128)(2,1)} copy(bf16[20,2,3,50,640]{4,1,3,2,0:T(2,128)(2,1)} %param.8) | data formatting | bytes 15360000 | tf_op args[1]
  49.6 0.9 multiply_multiply_fusion
  50.5 54.3 %shard_map.86 = (f32[20,2,3,50,640]{4,3,2,1,0:T(8,128)}, f32[5,32,8,1024]{3,2,1,0:T(8,128)}) custom-call(s32[640]{0:T(1024)} %order_ref.1, f32[20,2,3,50,640]{4,3,2,1,0:T(8,128)} %copy.33.old_ref, bf16[20,2,3,50,640]{4,3,2,1,0:T(8,128)(2,1)} %copy.34.noise_ref, f32[20,640,640]{2,1,0:T(8,128)} %basis_ref.1, f32[20,3,640]{2,1,0:T(4,128)} %get-tuple-element.37.keep_ref, ...), custom_call_target="tpu_custom_call" | custom-call | tf_op jit(solution)/shard_map/pallas_call | solution.py:123
  104.8 5.6 %copy.35 = f32[5,32,8,1024]{3,2,0,1:T(8,128)} copy(f32[5,32,8,1024]{3,2,1,0:T(8,128)} %get-tuple-element.5) | data formatting | bytes 10485760 | tf_op jit(solution)/shard_map/pallas_call | solution.py:123
  110.4 7.6 %all-to-all-start = ((f32[5,32,8,1024]{3,2,0,1:T(8,128)}), f32[5,32,8,1024]{3,2,0,1:T(8,128)}, u32[]{:S(2)}, u32[]{:S(2)}) async-start(f32[5,32,8,1024]{3,2,0,1:T(8,128)} %copy.35), calls=%async_computation | async-start | bytes 10485760 | tf_op jit(solution)/shard_map/all_to_all | solution.py:153
  118.3 14.0 %cosine_multiply_fusion = (f32[640,1,1280]{2,0,1:T(8,128)S(1)}, f32[640,1,1280]{2,0,1:T(8,128)S(1)}) fusion(s32[640]{0:T(1024)S(1)} %reshape.188, f32[640]{0:T(1024)S(1)} %get-tuple-element.40, f32[640]{0:T(1024)S(1)} %get-tuple-element.41), kind=kLoop, calls=%fused_computation.9 | loop fusion | flops 9011200 | bytes 6561280 | tf_op jit(solution)/shard_map/mul | solution.py:139
  132.3 3.2 %pad_maximum_fusion = f32[640,2,1280]{2,0,1:T(8,128)} fusion(f32[640,1,1280]{2,0,1:T(8,128)S(1)} %get-tuple-element.39, f32[640,1,1280]{2,0,1:T(8,128)S(1)} %get-tuple-element.38), kind=kLoop, calls=%fused_computation.2 | loop fusion | flops 1638400 | bytes 13107200 | tf_op jit(solution)/shard_map/stack | solution.py:139
  135.5 10.7 %copy.38 = f32[640,2,1280]{2,1,0:T(2,128)} copy(f32[640,2,1280]{2,0,1:T(8,128)} %pad_maximum_fusion) | data formatting | bytes 13107200 | tf_op jit(solution)/shard_map/stack | solution.py:139
  146.2 8.7 %reshape.189 = f32[1280,1280]{1,0:T(8,128)} reshape(f32[640,2,1280]{2,1,0:T(2,128)} %copy.38) | data formatting | bytes 13107200 | tf_op jit(solution)/shard_map/reshape | solution.py:139
  154.9 22.6 %copy.39 = f32[20,2,3,50,640]{4,1,3,2,0:T(2,128)} copy(f32[20,2,3,50,640]{4,3,2,1,0:T(8,128)} %get-tuple-element.24) | data formatting | bytes 30720000
  177.4 54.8 %all-to-all-done = f32[5,32,8,1024]{3,2,0,1:T(8,128)} async-done(((f32[5,32,8,1024]{3,2,0,1:T(8,128)}), f32[5,32,8,1024]{3,2,0,1:T(8,128)}, u32[]{:S(2)}, u32[]{:S(2)}) %all-to-all-start) | async-done | bytes 5242912 | tf_op jit(solution)/shard_map/all_to_all | solution.py:153
  232.3 3.3 %copy.36 = f32[5,32,8,1024]{3,2,1,0:T(8,128)S(1)} copy(f32[5,32,8,1024]{3,2,0,1:T(8,128)} %all-to-all-done) | data formatting | bytes 10485760 | tf_op jit(solution)/shard_map/all_to_all | solution.py:153
  235.6 1.1 copy-done
  236.7 14.2 %fusion = f32[1000,1280]{1,0:T(8,128)} fusion(f32[1280,1280]{1,0:T(8,128)S(1)} %copy-done, f32[1280,1024]{1,0:T(8,128)S(1)} %bitcast.12), kind=kOutput, calls=%fused_computation.3 | convolution fusion | flops 9830400000 | bytes 16916480 | tf_op jit(solution)/shard_map/dot_general | solution.py:157
  250.9 6.6 %reshape.190 = f32[20,50,1280]{2,1,0:T(8,128)} reshape(f32[1000,1280]{1,0:T(8,128)} %fusion) | data formatting | bytes 10240000 | tf_op jit(solution)/shard_map/reshape | solution.py:158
  (60 shorter events, 17.9 us)
Async XLA Ops:
  41.8 7.8 %copy-start.2 = (f32[3]{0:T(128)S(1)}, f32[3]{0:T(128)}, u32[]{:S(2)}) copy-start(f32[3]{0:T(128)} %param.10) | copy-start | bytes 40
  110.4 7.6 %copy-start.1 = (s32[640]{0:T(1024)S(1)}, s32[640]{0:T(1024)}, u32[]{:S(2)}) copy-start(s32[640]{0:T(1024)} %param.12) | copy-start | bytes 7684
  110.4 121.8 %all-to-all-start = ((f32[5,32,8,1024]{3,2,0,1:T(8,128)}), f32[5,32,8,1024]{3,2,0,1:T(8,128)}, u32[]{:S(2)}, u32[]{:S(2)}) async-start(f32[5,32,8,1024]{3,2,0,1:T(8,128)} %copy.35), calls=%async_computation | async-start | bytes 10485760 | tf_op jit(solution)/shard_map/all_to_all | solution.py:153
  232.3 4.4 %copy-start = (f32[1280,1280]{1,0:T(8,128)S(1)}, f32[1280,1280]{1,0:T(8,128)}, u32[]{:S(2)}) copy-start(f32[1280,1280]{1,0:T(8,128)} %reshape.189) | copy-start | bytes 19660804
